TPU v7x, 128 devices: a whole 4x4x4 slice. The times are simulated.
128 devices in a mesh: dp: 1, ep: 128 (over z, y, x, core).
Axes of the slice: x: 4, y: 4, z: 4, core: 2. Of those that a mesh axis runs over, the one named last changes fastest.
Arguments:
- tokens: bfloat16 [65536, 2048], P(('dp', 'ep'))
- choice_idx: int32 [128, 1024], P(('dp', 'ep'))
- gate_weight: float32 [128, 1024], P(('dp', 'ep'))
- w_in: bfloat16 [128, 2048, 768], P('ep')
- w_out: bfloat16 [128, 768, 2048], P('ep')
Outputs:
- output: bfloat16 [65536, 2048], P(('dp', 'ep'))
All inputs are finite; a program needn't handle non-finite values.
Results may differ from a plain program's by a relative error of at most 0.00638937.
Values are sent between devices in bfloat16 or wider.
A program may use at most 1 GiB of HBM per device.

v0:
```python
import jax
import jax.numpy as jnp
from jax import lax
from jax.sharding import PartitionSpec as P


def solution(mesh):
    group_n = mesh.shape["ep"]
    row_spec = P(("dp", "ep"), None)
    expert_spec = P("ep", None, None)

    def local_layer(tok_loc, sel_loc, gate_loc, win_loc, wout_loc):
        tok_count, model_dim = tok_loc.shape
        exp_count, cap_slots = sel_loc.shape
        slot_total = exp_count * cap_slots
        pair_cap = 2 * slot_total // group_n
        flat_sel = sel_loc.reshape(slot_total)
        src_dev = flat_sel // tok_count
        src_row = flat_sel % tok_count
        slot_order = jnp.argsort(src_dev, stable=True)
        counts = jax.ops.segment_sum(jnp.ones_like(src_dev), src_dev, num_segments=group_n)
        starts = jnp.cumsum(counts) - counts
        lane_idx = jnp.arange(pair_cap, dtype=jnp.int32)
        is_valid = lane_idx[None, :] < counts[:, None]
        slot_of = slot_order[jnp.minimum(starts[:, None] + lane_idx[None, :], slot_total - 1)]
        request = jnp.where(is_valid, src_row[slot_of], 0)
        sorted_rank = jnp.zeros(slot_total, jnp.int32).at[slot_order].set(jnp.arange(slot_total, dtype=jnp.int32))
        recv_place = src_dev * pair_cap + sorted_rank - starts[src_dev]
        asked_rows = lax.all_to_all(request, "ep", 0, 0, tiled=True)
        send_rows = tok_loc[asked_rows]
        got_rows = lax.all_to_all(send_rows, "ep", 0, 0, tiled=True)
        expert_in = got_rows.reshape(group_n * pair_cap, model_dim)[recv_place].reshape(exp_count, cap_slots, model_dim)
        pre_act = jnp.einsum("ecd,edf->ecf", expert_in, win_loc, preferred_element_type=jnp.float32)
        hidden = jax.nn.gelu(pre_act, approximate=True).astype(jnp.bfloat16)
        expert_out = jnp.einsum("ecf,efd->ecd", hidden, wout_loc, preferred_element_type=jnp.float32)
        weighted = (gate_loc[:, :, None] * expert_out).astype(jnp.bfloat16).reshape(slot_total, model_dim)
        back_rows = jnp.where(is_valid[:, :, None], weighted[slot_of], jnp.zeros((), jnp.bfloat16))
        returned = lax.all_to_all(back_rows, "ep", 0, 0, tiled=True)
        added = jax.ops.segment_sum(returned.reshape(group_n * pair_cap, model_dim).astype(jnp.float32), asked_rows.reshape(group_n * pair_cap), num_segments=tok_count)
        return (tok_loc.astype(jnp.float32) + added).astype(jnp.bfloat16)

    return jax.shard_map(local_layer, mesh=mesh, in_specs=(row_spec, row_spec, row_spec, expert_spec, expert_spec), out_specs=row_spec, check_vma=False)
```

profile of v0, /device:TPU:12, one launch (start us, length us, event | category | flops | bytes accessed | tf_op | source)
XLA Modules:
  0.0 411.3 jit_solution(8075106794549621058)
XLA Ops:
  0.0 0.0 copy-start
  0.0 0.0 copy-start.1
  0.0 0.9 compare_select_fusion.3
  0.9 7.6 %scatter_custom_fusion = s32[128]{0:T(128)S(1)} fusion(s32[1024]{0:T(1024)S(1)} %bitcast.46, s32[1024]{0:T(1024)S(1)} %broadcast.233, s32[]{:T(128)} %constant.18.clone.1), kind=kCustom, calls=%fused_computation.54 | custom fusion | flops 1024 | bytes 516 | tf_op jit(solution)/shard_map/scatter-add | solution.py:21
  8.5 0.1 copy.8
  8.6 0.2 reduce-window.9
  8.8 0.1 reduce
  8.9 0.1 compare_select_fusion.2
  9.0 6.6 %gather_fusion.3 = s32[1024]{0:T(1024)S(1)} fusion(s32[128]{0:T(128)S(1)} %sub.19, s32[1024]{0:T(1024)S(1)} %broadcast_clamp_fusion.3), kind=kCustom, calls=%fused_computation.3 | custom fusion | bytes 12288 | tf_op jit(solution)/shard_map/gather | solution.py:28
  15.6 0.0 copy-done.1
  15.6 4.4 %sort.17 = (s32[1024]{0:T(1024)}, s32[1024]{0:T(1024)S(1)}) sort(s32[1024]{0:T(1024)S(1)} %add_select_fusion, s32[1024]{0:T(1024)S(1)} %iota.20), dimensions={0}, to_apply=%region_1.2 | sort | flops 10240 | bytes 16384 | tf_op jit(solution)/shard_map/jit(argsort)/sort | solution.py:20
  20.0 0.1 reshape.309
  20.1 8.6 %gather_fusion = s32[2048]{0:T(1024)S(1)} fusion(s32[1024]{0:T(1024)S(1)} %get-tuple-element.6, s32[2048]{0:T(1024)S(1)} %broadcast_clamp_fusion.1), kind=kCustom, calls=%fused_computation | custom fusion | bytes 24576 | tf_op jit(solution)/shard_map/gather | solution.py:25
  28.7 0.1 gather.23
  28.8 0.1 reshape.317
  28.9 4.3 %scatter_custom_fusion.1 = s32[1024]{0:T(1024)S(1)} fusion(s32[1024]{0:T(1024)S(1)} %compare_select_fusion.5, s32[1024]{0:T(1024)S(1)} %iota.21, s32[]{:T(128)} %constant.18.clone.1), kind=kCustom, calls=%fused_computation.52 | custom fusion | bytes 4100 | tf_op jit(solution)/shard_map/scatter | solution.py:27
  33.2 8.6 %gather_fusion.1 = s32[2048]{0:T(1024)S(1)} fusion(s32[1024]{0:T(1024)S(1)} %get-tuple-element.10, s32[2048]{0:T(1024)S(1)} %broadcast_clamp_fusion.2), kind=kCustom, calls=%fused_computation.1 | custom fusion | bytes 24576 | tf_op jit(solution)/shard_map/gather | solution.py:26
  41.8 0.1 gather.25
  41.9 0.1 fusion.17
  42.0 17.8 %all_to_all.19 = s32[128,1,16]{2,1,0:T(1,128)S(1)} all-to-all(s32[128,1,16]{2,1,0:T(1,128)S(1)} %bitcast.41), channel_id=1, replica_groups=mesh['dp'=1,'ep'=128] {'ep'}, dimensions={0} | all-to-all | bytes 16384 | tf_op jit(solution)/shard_map/all_to_all | solution.py:29
  59.8 0.1 reshape.325
  59.9 18.2 %gather_fusion.2 = bf16[2048,2048]{1,0:T(8,128)(2,1)} fusion(bf16[512,2048]{1,0:T(8,128)(2,1)} %param.5, s32[2048]{0:T(1024)S(1)} %broadcast_clamp_fusion), kind=kCustom, calls=%fused_computation.2 | custom fusion | bytes 16785408 | tf_op jit(solution)/shard_map/gather | solution.py:30
  78.1 7.9 %all-to-all-start.1 = ((bf16[128,16,2048]{2,1,0:T(8,128)(2,1)}), bf16[128,16,2048]{2,1,0:T(8,128)(2,1)}, u32[]{:S(2)}, u32[]{:S(2)}) async-start(bf16[128,16,2048]{2,1,0:T(8,128)(2,1)} %bitcast.39), calls=%async_computation.1 | async-start | bytes 16777216 | tf_op jit(solution)/shard_map/all_to_all | solution.py:31
  86.0 0.1 iota_compare_fusion
  86.1 108.7 %all-to-all-done.1 = bf16[128,16,2048]{2,1,0:T(8,128)(2,1)} async-done(((bf16[128,16,2048]{2,1,0:T(8,128)(2,1)}), bf16[128,16,2048]{2,1,0:T(8,128)(2,1)}, u32[]{:S(2)}, u32[]{:S(2)}) %all-to-all-start.1) | async-done | bytes 8388640 | tf_op jit(solution)/shard_map/all_to_all | solution.py:31
  194.7 0.0 copy-start.2
  194.7 13.3 %gather_fusion.4 = bf16[1024,2048]{1,0:T(8,128)(2,1)} fusion(bf16[2048,2048]{1,0:T(8,128)(2,1)} %bitcast.8, s32[1024]{0:T(1024)S(1)} %get-tuple-element.9), kind=kCustom, calls=%fused_computation.4 | custom fusion | bytes 8392704 | tf_op jit(solution)/shard_map/gather | solution.py:32
  208.1 0.0 copy-done
  208.1 0.0 copy-done.2
  208.1 11.9 %multiply_convert_fusion = bf16[1024,2048]{1,0:T(8,128)(2,1)} fusion(f32[1024]{0:T(1024)S(1)} %bitcast.47, bf16[1,768,2048]{2,1,0:T(8,128)(2,1)S(1)} %copy-done, bf16[1024,2048]{1,0:T(8,128)(2,1)} %gather_fusion.4, bf16[1,2048,768]{2,1,0:T(8,128)(2,1)} %param.8), kind=kOutput, calls=%fused_computation.11 | convolution fusion | flops 6453723136 | bytes 14684160 | tf_op jit(solution)/shard_map/ecf,efd->ecd/dot_general | solution.py:35
  220.0 19.1 %gather_fusion.5 = bf16[2048,2048]{1,0:T(8,128)(2,1)} fusion(bf16[1024,2048]{1,0:T(8,128)(2,1)} %multiply_convert_fusion, s32[2048]{0:T(1024)S(1)} %broadcast_clamp_fusion.2), kind=kCustom, calls=%fused_computation.5 | custom fusion | bytes 16785408 | tf_op jit(solution)/shard_map/gather | solution.py:37
  239.0 7.3 %broadcast_select_fusion = bf16[128,16,2048]{2,1,0:T(8,128)(2,1)} fusion(bf16[128,16,2048]{2,1,0:T(8,128)(2,1)} %bitcast.38, pred[128,16]{1,0:T(8,128)(4,1)S(1)} %iota_compare_fusion), kind=kLoop, calls=%fused_computation.12 | loop fusion | flops 4194304 | bytes 16779264 | tf_op jit(solution)/shard_map/jit(_where)/select_n | solution.py:37
  246.3 13.2 %all-to-all-start.2 = ((bf16[128,16,2048]{2,1,0:T(8,128)(2,1)}), bf16[128,16,2048]{2,1,0:T(8,128)(2,1)}, u32[]{:S(2)}, u32[]{:S(2)}) async-start(bf16[128,16,2048]{2,1,0:T(8,128)(2,1)} %broadcast_select_fusion), calls=%async_computation.2 | async-start | bytes 16777216 | tf_op jit(solution)/shard_map/all_to_all | solution.py:38
  259.4 4.0 convert_element_type.20
  263.5 0.5 broadcast.283
  264.0 0.8 reduce.4
  264.8 0.1 reshape.373
  264.9 110.9 %all-to-all-done.2 = bf16[128,16,2048]{2,1,0:T(8,128)(2,1)} async-done(((bf16[128,16,2048]{2,1,0:T(8,128)(2,1)}), bf16[128,16,2048]{2,1,0:T(8,128)(2,1)}, u32[]{:S(2)}, u32[]{:S(2)}) %all-to-all-start.2) | async-done | bytes 8388640 | tf_op jit(solution)/shard_map/all_to_all | solution.py:38
  375.8 31.7 %scatter_custom_fusion.2 = f32[512,2048]{1,0:T(8,128)} fusion(f32[512,2048]{1,0:T(8,128)} %convert_element_type.20, s32[2048]{0:T(1024)S(1)} %reshape.373, bf16[2048,2048]{1,0:T(8,128)(2,1)} %bitcast.14), kind=kCustom, calls=%fused_computation.9 | custom fusion | flops 8388608 | bytes 12582912 | tf_op jit(solution)/shard_map/scatter-add | solution.py:39
  407.4 3.8 convert_element_type.25
  (13 shorter events, 0.1 us)
Async XLA Ops:
  0.0 208.1 %copy-start = (bf16[1,768,2048]{2,1,0:T(8,128)(2,1)S(1)}, bf16[1,768,2048]{2,1,0:T(8,128)(2,1)}, u32[]{:S(2)}) copy-start(bf16[1,768,2048]{2,1,0:T(8,128)(2,1)} %param.9) | copy-start | bytes 9437188
  0.0 15.6 %copy-start.1 = (s32[1,1024]{1,0:T(1,128)S(1)}, s32[1,1024]{1,0:T(1,128)}, u32[]{:S(2)}) copy-start(s32[1,1024]{1,0:T(1,128)} %param.6) | copy-start | bytes 12292
  78.1 116.6 %all-to-all-start.1 = ((bf16[128,16,2048]{2,1,0:T(8,128)(2,1)}), bf16[128,16,2048]{2,1,0:T(8,128)(2,1)}, u32[]{:S(2)}, u32[]{:S(2)}) async-start(bf16[128,16,2048]{2,1,0:T(8,128)(2,1)} %bitcast.39), calls=%async_computation.1 | async-start | bytes 16777216 | tf_op jit(solution)/shard_map/all_to_all | solution.py:31
  194.7 13.3 %copy-start.2 = (f32[1,1024]{1,0:T(1,128)S(1)}, f32[1,1024]{1,0:T(1,128)}, u32[]{:S(2)}) copy-start(f32[1,1024]{1,0:T(1,128)} %param.7) | copy-start | bytes 12292
  246.3 129.5 %all-to-all-start.2 = ((bf16[128,16,2048]{2,1,0:T(8,128)(2,1)}), bf16[128,16,2048]{2,1,0:T(8,128)(2,1)}, u32[]{:S(2)}, u32[]{:S(2)}) async-start(bf16[128,16,2048]{2,1,0:T(8,128)(2,1)} %broadcast_select_fusion), calls=%async_computation.2 | async-start | bytes 16777216 | tf_op jit(solution)/shard_map/all_to_all | solution.py:38
where the time goes:
time: 412 us; the launch traced here: 411 us
  waiting for transfers between devices  220 us (53%)
  local copies, waits for them, and re-layouts  79.7 us (19%)
  other arithmetic  61 us (15%)
  starting transfers between devices  21 us (5%)
  blocking collectives  17.8 us (4%)
  matrix products  11.9 us (3%)
    all_to_all x1, waiting for transfers between devices, local_layer(): returned = lax.all_to_all(back_rows, 'ep', 0, 0, tiled=True)  111 us
    all_to_all x1, waiting for transfers between devices, local_layer(): got_rows = lax.all_to_all(send_rows, 'ep', 0, 0, tiled=True)  109 us
    scatter-add x1, other arithmetic, local_layer(): jax.ops.segment_sum(returned.reshape(group_n * pair_cap, model_dim).astyp...  31.7 us
    gather x1, local copies, waits for them, and re-layouts, local_layer(): weighted[slot_of]  19.1 us
    gather x1, local copies, waits for them, and re-layouts, local_layer(): send_rows = tok_loc[asked_rows]  18.2 us
    all_to_all x1, blocking collectives, local_layer(): asked_rows = lax.all_to_all(request, 'ep', 0, 0, tiled=True)  17.8 us
    gather x1, local copies, waits for them, and re-layouts, local_layer(): got_rows.reshape(group_n * pair_cap, model_dim)[recv_place]  13.3 us
    all_to_all x1, starting transfers between devices, local_layer(): returned = lax.all_to_all(back_rows, 'ep', 0, 0, tiled=True)  13.2 us
  transfers between devices with their start and end apart: 2, of which 2 were waited for; matrix products, arithmetic and copies ran while one was open for 1% of the time, Pallas kernels for 0%

commit v1 on v0

v1 whole, which is shorter than its diff:
```python
import functools

import jax
import jax.numpy as jnp
from jax import lax
from jax.experimental import pallas as pl
from jax.experimental.pallas import tpu as pltpu
from jax.sharding import PartitionSpec as P

MESH = pl.DeviceIdType.MESH
HIGHEST = lax.Precision.HIGHEST
PEERS = 8
LANES = 128


def _dot(a, b, dims=((1,), (0,)), precision=None):
    return lax.dot_general(a, b, (dims, ((), ())), precision=precision, preferred_element_type=jnp.float32)


def moe_kernel(n, sel_ref, gate_ref, tok_hbm, win_hbm, wout_hbm, out_ref,
               tok, win, wout, ask_out, ask_in, gates, rows_out, rows_in, back_out, back_in, acc,
               load_sem, ask_send, ask_recv, rows_send, rows_recv, back_send, back_recv):
    me = lax.axis_index("ep")
    groups = n // PEERS
    my_group = me // PEERS
    pair_cap = LANES // PEERS
    tok_count, model_dim = tok.shape
    slots = sel_ref.shape[1]

    loads = [
        pltpu.make_async_copy(src, dst, load_sem.at[i])
        for i, (src, dst) in enumerate(((tok_hbm, tok), (win_hbm, win), (wout_hbm, wout)))
    ]
    for load in loads:
        load.start()

    barrier = pltpu.get_barrier_semaphore()

    @pl.loop(1, n)
    def _(k):
        pl.semaphore_signal(barrier, inc=1, device_id={"ep": (me + k) % n}, device_id_type=MESH)

    shift = tok_count.bit_length() - 1
    upper = (lax.broadcasted_iota(jnp.int32, (LANES, LANES), 0)
             < lax.broadcasted_iota(jnp.int32, (LANES, LANES), 1)).astype(jnp.bfloat16)
    lane_of = lax.broadcasted_iota(jnp.int32, (LANES, LANES), 0) % pair_cap
    before = jnp.zeros((n, 1), jnp.float32)
    asks = jnp.zeros((n, LANES), jnp.float32)
    weights = jnp.zeros((n, LANES), jnp.float32)
    for b in range(slots // LANES):
        part = slice(b * LANES, (b + 1) * LANES)
        sel = sel_ref[:, part]
        dev = lax.shift_right_logical(sel, shift)
        row = (sel & (tok_count - 1)).astype(jnp.float32) + 1.0
        hot = lax.broadcasted_iota(jnp.int32, (n, LANES), 0) == dev
        hot_f = hot.astype(jnp.float32)
        count = _dot(hot_f.astype(jnp.bfloat16), upper) + before
        before = before + jnp.sum(hot_f, axis=1, keepdims=True)
        rank = jnp.sum(hot_f * count, axis=0, keepdims=True).astype(jnp.int32)
        mine = lane_of == rank
        asks = asks + _dot(hot_f, jnp.where(mine, row, 0.0), ((1,), (1,)), HIGHEST)
        weights = weights + _dot(hot_f, jnp.where(mine, gate_ref[:, part], 0.0), ((1,), (1,)), HIGHEST)
    gates[...] = weights
    ask_out[...] = asks.reshape(n, 1, LANES)

    pl.semaphore_wait(barrier, n - 1)

    @pl.loop(1, n)
    def _(k):
        peer = (me + k) % n
        pltpu.make_async_remote_copy(
            src_ref=ask_out.at[peer], dst_ref=ask_in.at[me], send_sem=ask_send, recv_sem=ask_recv,
            device_id={"ep": peer}, device_id_type=MESH).start()

    pltpu.make_async_copy(ask_out.at[me], ask_in.at[me], ask_recv).start()

    pltpu.make_async_copy(ask_in, ask_in, ask_recv).wait()
    for load in loads:
        load.wait()

    own_lanes = (lax.broadcasted_iota(jnp.int32, (PEERS, LANES), 1) // pair_cap
                 == lax.broadcasted_iota(jnp.int32, (PEERS, LANES), 0))

    def lane_row(block):
        return jnp.sum(jnp.where(own_lanes, block, 0.0), axis=0, keepdims=True)

    def column(line):
        return jnp.transpose(jnp.broadcast_to(line, (LANES, LANES)))

    def asked(group):
        return lane_row(ask_in[pl.ds(group * PEERS, PEERS)].reshape(PEERS, LANES))

    def push(src, dst, group, send_sem, recv_sem):
        for i in range(PEERS):
            peer = group * PEERS + i

            @pl.when(peer != me)
            def _():
                pltpu.make_async_remote_copy(
                    src_ref=src.at[peer], dst_ref=dst.at[me], send_sem=send_sem, recv_sem=recv_sem.at[my_group],
                    device_id={"ep": peer}, device_id_type=MESH).start()

            @pl.when(peer == me)
            def _():
                pltpu.make_async_copy(src.at[me], dst.at[me], recv_sem.at[my_group]).start()

    def arrived(dst, group, recv_sem):
        blocks = dst.at[pl.ds(group * PEERS, PEERS)]
        pltpu.make_async_copy(blocks, blocks, recv_sem.at[group]).wait()

    def later(j):
        return (my_group + j) % groups

    def earlier(j):
        return (my_group + groups - j) % groups

    row_ids = lax.broadcasted_iota(jnp.int32, (LANES, tok_count), 1).astype(jnp.float32) + 1.0

    @pl.loop(0, groups)
    def _(j):
        group = later(j)
        want = column(asked(group))
        pick = (jnp.concatenate([want] * (tok_count // LANES), axis=1) == row_ids).astype(jnp.bfloat16)
        for c in range(0, model_dim, 512):
            got = _dot(pick, tok[:, c:c + 512]).astype(jnp.bfloat16)
            rows_out[pl.ds(group * PEERS, PEERS), :, c:c + 512] = got.reshape(PEERS, pair_cap, 512)
        push(rows_out, rows_in, group, rows_send, rows_recv)

    @pl.loop(0, groups)
    def _(j):
        group = earlier(j)
        arrived(rows_in, group, rows_recv)
        first = pl.ds(group * PEERS, PEERS)
        x = rows_in[first].reshape(LANES, model_dim)
        hidden = jax.nn.gelu(_dot(x, win[...]), approximate=True).astype(jnp.bfloat16)
        scale = column(lane_row(gates[pl.ds(pl.multiple_of(group * PEERS, PEERS), PEERS), :]))
        scale = jnp.concatenate([scale] * (512 // LANES), axis=1)
        for c in range(0, model_dim, 512):
            o = _dot(hidden, wout[:, c:c + 512])
            p = jnp.where(scale > 0.0, scale * o, 0.0).astype(jnp.bfloat16)
            back_out[first, :, c:c + 512] = p.reshape(PEERS, pair_cap, 512)
        push(back_out, back_in, group, back_send, back_recv)

    token_ids = lax.broadcasted_iota(jnp.int32, (tok_count, LANES), 0).astype(jnp.float32) + 1.0

    for c in range(0, model_dim, 512):
        acc[:, c:c + 512] = tok[:, c:c + 512].astype(jnp.float32)

    @pl.loop(0, groups)
    def _(j):
        group = later(j)
        put = (token_ids == asked(group)).astype(jnp.bfloat16)
        arrived(back_in, group, back_recv)
        for c in range(0, model_dim, 512):
            p = back_in[pl.ds(group * PEERS, PEERS), :, c:c + 512].reshape(LANES, 512)
            acc[:, c:c + 512] += _dot(put, p)

    for c in range(0, model_dim, 512):
        out_ref[:, c:c + 512] = acc[:, c:c + 512].astype(out_ref.dtype)

    for src, send_sem in ((ask_out, ask_send), (rows_out, rows_send), (back_out, back_send)):
        sent = src.at[pl.ds(0, n - 1)]
        pltpu.make_async_copy(sent, sent, send_sem).wait()


def solution(mesh):
    n = mesh.shape["ep"]
    row_spec = P(("dp", "ep"), None)
    expert_spec = P("ep", None, None)

    def local_layer(tok_loc, sel_loc, gate_loc, win_loc, wout_loc):
        tok_count, model_dim = tok_loc.shape
        ff_dim = win_loc.shape[2]
        pair_cap = LANES // PEERS
        blocks = pltpu.VMEM((n, pair_cap, model_dim), jnp.bfloat16)
        vmem = pl.BlockSpec(memory_space=pltpu.VMEM)
        hbm = pl.BlockSpec(memory_space=pl.ANY)
        return pl.pallas_call(
            functools.partial(moe_kernel, n),
            out_shape=jax.ShapeDtypeStruct((tok_count, model_dim), tok_loc.dtype),
            in_specs=[vmem, vmem, hbm, hbm, hbm],
            out_specs=vmem,
            scratch_shapes=[
                pltpu.VMEM((tok_count, model_dim), jnp.bfloat16),
                pltpu.VMEM((model_dim, ff_dim), jnp.bfloat16),
                pltpu.VMEM((ff_dim, model_dim), jnp.bfloat16),
                pltpu.VMEM((n, 1, LANES), jnp.float32),
                pltpu.VMEM((n, 1, LANES), jnp.float32),
                pltpu.VMEM((n, LANES), jnp.float32),
                blocks, blocks, blocks, blocks,
                pltpu.VMEM((tok_count, model_dim), jnp.float32),
                pltpu.SemaphoreType.DMA((3,)),
                pltpu.SemaphoreType.DMA,
                pltpu.SemaphoreType.DMA,
                pltpu.SemaphoreType.DMA,
                pltpu.SemaphoreType.DMA((n // PEERS,)),
                pltpu.SemaphoreType.DMA,
                pltpu.SemaphoreType.DMA((n // PEERS,)),
            ],
            compiler_params=pltpu.CompilerParams(
                collective_id=0, has_side_effects=True, vmem_limit_bytes=63 * 1024 * 1024),
        )(sel_loc, gate_loc, tok_loc, win_loc[0], wout_loc[0])

    return jax.shard_map(local_layer, mesh=mesh, in_specs=(row_spec, row_spec, row_spec, expert_spec, expert_spec), out_specs=row_spec, check_vma=False)
```

time: 412 us -> 288 us (0.70)
  the two profiles are of different devices: /device:TPU:12 before, /device:TPU:47 now
where the time goes in v1:
time: 288 us
  Pallas kernels  285 us (99%)
  local copies, waits for them, and re-layouts  3.16 us (1%)
    pallas_call x1, Pallas kernels, local_layer(): pl.pallas_call(functools.partial(moe_kernel, n), out_shape=jax.ShapeDtype...  285 us

profile of v1, /device:TPU:47, one launch (start us, length us, event | category | flops | bytes accessed | tf_op | source)
XLA Modules:
  0.0 287.8 jit_solution(18228243291515998084)
XLA Ops:
  0.0 284.6 %shard_map.55 = bf16[512,2048]{1,0:T(8,128)(2,1)} custom-call(s32[1,1024]{1,0:T(1,128)} %sel_ref.1, f32[1,1024]{1,0:T(1,128)} %gate_ref.1, bf16[512,2048]{1,0:T(8,128)(2,1)} %tok_hbm.1, bf16[2048,768]{1,0:T(8,128)(2,1)} %bitcast.2, bf16[768,2048]{1,0:T(8,128)(2,1)} %bitcast.3), custom_call_target="tpu_custom_call" | custom-call | tf_op jit(solution)/shard_map/pallas_call | solution.py:178
  284.6 3.2 %copy.7 = bf16[512,2048]{1,0:T(8,128)(2,1)} copy(bf16[512,2048]{1,0:T(8,128)(2,1)} %shard_map.55) | data formatting | bytes 4194304

commit v2 on v1

--- a/solution.py
+++ b/solution.py
@@ -22,7 +22,6 @@
                load_sem, ask_send, ask_recv, rows_send, rows_recv, back_send, back_recv):
     me = lax.axis_index("ep")
     groups = n // PEERS
-    my_group = me // PEERS
     pair_cap = LANES // PEERS
     tok_count, model_dim = tok.shape
     slots = sel_ref.shape[1]
@@ -33,6 +32,32 @@
     ]
     for load in loads:
         load.start()
+
+    ys = min(4, n // 8)
+    zs = n // (8 * ys)
+
+    def partner(j, i, sign):
+        t, core = i // 2, i % 2
+        y_shift, z_shift = j % ys + t, j // ys + 4 - t
+        x = (me // 2 + 4 + sign * t) % 4
+        y = (me // 8 + 8 + sign * y_shift) % ys
+        z = (me // (8 * ys) + 8 + sign * z_shift) % zs
+        return ((z * ys + y) * 4 + x) * 2 + (me + core) % 2
+
+    def push(src, dst, j, i, peer, index, send_sem, recv_sem):
+        def remote():
+            pltpu.make_async_remote_copy(
+                src_ref=src.at[index], dst_ref=dst.at[j * PEERS + i], send_sem=send_sem, recv_sem=recv_sem,
+                device_id={"ep": peer}, device_id_type=MESH).start()
+
+        def local():
+            pltpu.make_async_copy(src.at[index], dst.at[j * PEERS + i], recv_sem).start()
+
+        if i > 0:
+            remote()
+        else:
+            pl.when(j > 0)(remote)
+            pl.when(j == 0)(local)
 
     barrier = pltpu.get_barrier_semaphore()
 
@@ -60,19 +85,15 @@
         mine = lane_of == rank
         asks = asks + _dot(hot_f, jnp.where(mine, row, 0.0), ((1,), (1,)), HIGHEST)
         weights = weights + _dot(hot_f, jnp.where(mine, gate_ref[:, part], 0.0), ((1,), (1,)), HIGHEST)
-    gates[...] = weights
+    gates[...] = weights.reshape(n, 1, LANES)
     ask_out[...] = asks.reshape(n, 1, LANES)
 
     pl.semaphore_wait(barrier, n - 1)
 
-    @pl.loop(1, n)
-    def _(k):
-        peer = (me + k) % n
-        pltpu.make_async_remote_copy(
-            src_ref=ask_out.at[peer], dst_ref=ask_in.at[me], send_sem=ask_send, recv_sem=ask_recv,
-            device_id={"ep": peer}, device_id_type=MESH).start()
-
-    pltpu.make_async_copy(ask_out.at[me], ask_in.at[me], ask_recv).start()
+    @pl.loop(0, groups)
+    def _(j):
+        for i in range(PEERS):
+            push(ask_out, ask_in, j, i, partner(j, i, -1), partner(j, i, -1), ask_send, ask_recv)
 
     pltpu.make_async_copy(ask_in, ask_in, ask_recv).wait()
     for load in loads:
@@ -87,59 +108,40 @@
     def column(line):
         return jnp.transpose(jnp.broadcast_to(line, (LANES, LANES)))
 
-    def asked(group):
-        return lane_row(ask_in[pl.ds(group * PEERS, PEERS)].reshape(PEERS, LANES))
-
-    def push(src, dst, group, send_sem, recv_sem):
-        for i in range(PEERS):
-            peer = group * PEERS + i
-
-            @pl.when(peer != me)
-            def _():
-                pltpu.make_async_remote_copy(
-                    src_ref=src.at[peer], dst_ref=dst.at[me], send_sem=send_sem, recv_sem=recv_sem.at[my_group],
-                    device_id={"ep": peer}, device_id_type=MESH).start()
-
-            @pl.when(peer == me)
-            def _():
-                pltpu.make_async_copy(src.at[me], dst.at[me], recv_sem.at[my_group]).start()
+    def asked(j):
+        return lane_row(ask_in[pl.ds(j * PEERS, PEERS)].reshape(PEERS, LANES))
 
     def arrived(dst, group, recv_sem):
         blocks = dst.at[pl.ds(group * PEERS, PEERS)]
         pltpu.make_async_copy(blocks, blocks, recv_sem.at[group]).wait()
 
-    def later(j):
-        return (my_group + j) % groups
-
-    def earlier(j):
-        return (my_group + groups - j) % groups
-
     row_ids = lax.broadcasted_iota(jnp.int32, (LANES, tok_count), 1).astype(jnp.float32) + 1.0
 
     @pl.loop(0, groups)
     def _(j):
-        group = later(j)
-        want = column(asked(group))
+        want = column(asked(j))
         pick = (jnp.concatenate([want] * (tok_count // LANES), axis=1) == row_ids).astype(jnp.bfloat16)
         for c in range(0, model_dim, 512):
             got = _dot(pick, tok[:, c:c + 512]).astype(jnp.bfloat16)
-            rows_out[pl.ds(group * PEERS, PEERS), :, c:c + 512] = got.reshape(PEERS, pair_cap, 512)
-        push(rows_out, rows_in, group, rows_send, rows_recv)
-
-    @pl.loop(0, groups)
-    def _(j):
-        group = earlier(j)
-        arrived(rows_in, group, rows_recv)
-        first = pl.ds(group * PEERS, PEERS)
+            rows_out[pl.ds(j * PEERS, PEERS), :, c:c + 512] = got.reshape(PEERS, pair_cap, 512)
+        for i in range(PEERS):
+            push(rows_out, rows_in, j, i, partner(j, i, 1), j * PEERS + i, rows_send, rows_recv.at[j])
+
+    @pl.loop(0, groups)
+    def _(j):
+        arrived(rows_in, j, rows_recv)
+        first = pl.ds(j * PEERS, PEERS)
         x = rows_in[first].reshape(LANES, model_dim)
         hidden = jax.nn.gelu(_dot(x, win[...]), approximate=True).astype(jnp.bfloat16)
-        scale = column(lane_row(gates[pl.ds(pl.multiple_of(group * PEERS, PEERS), PEERS), :]))
+        lines = [gates[partner(j, i, -1)] for i in range(PEERS)]
+        scale = column(lane_row(jnp.concatenate(lines, axis=0)))
         scale = jnp.concatenate([scale] * (512 // LANES), axis=1)
         for c in range(0, model_dim, 512):
             o = _dot(hidden, wout[:, c:c + 512])
             p = jnp.where(scale > 0.0, scale * o, 0.0).astype(jnp.bfloat16)
             back_out[first, :, c:c + 512] = p.reshape(PEERS, pair_cap, 512)
-        push(back_out, back_in, group, back_send, back_recv)
+        for i in range(PEERS):
+            push(back_out, back_in, j, i, partner(j, i, -1), j * PEERS + i, back_send, back_recv.at[j])
 
     token_ids = lax.broadcasted_iota(jnp.int32, (tok_count, LANES), 0).astype(jnp.float32) + 1.0
 
@@ -148,11 +150,10 @@
 
     @pl.loop(0, groups)
     def _(j):
-        group = later(j)
-        put = (token_ids == asked(group)).astype(jnp.bfloat16)
-        arrived(back_in, group, back_recv)
+        put = (token_ids == asked(j)).astype(jnp.bfloat16)
+        arrived(back_in, j, back_recv)
         for c in range(0, model_dim, 512):
-            p = back_in[pl.ds(group * PEERS, PEERS), :, c:c + 512].reshape(LANES, 512)
+            p = back_in[pl.ds(j * PEERS, PEERS), :, c:c + 512].reshape(LANES, 512)
             acc[:, c:c + 512] += _dot(put, p)
 
     for c in range(0, model_dim, 512):
@@ -186,7 +187,7 @@
                 pltpu.VMEM((ff_dim, model_dim), jnp.bfloat16),
                 pltpu.VMEM((n, 1, LANES), jnp.float32),
                 pltpu.VMEM((n, 1, LANES), jnp.float32),
-                pltpu.VMEM((n, LANES), jnp.float32),
+                pltpu.VMEM((n, 1, LANES), jnp.float32),
                 blocks, blocks, blocks, blocks,
                 pltpu.VMEM((tok_count, model_dim), jnp.float32),
                 pltpu.SemaphoreType.DMA((3,)),

time: 288 us -> 284 us (0.986)
  the two profiles are of different devices: /device:TPU:47 before, /device:TPU:83 now
where the time goes in v2:
time: 284 us
  Pallas kernels  281 us (99%)
  local copies, waits for them, and re-layouts  3.16 us (1%)
    pallas_call x1, Pallas kernels, local_layer(): pl.pallas_call(functools.partial(moe_kernel, n), out_shape=jax.ShapeDtype...  281 us

profile of v2, /device:TPU:83, one launch (start us, length us, event | category | flops | bytes accessed | tf_op | source)
XLA Modules:
  0.0 284.0 jit_solution(14827174289726566993)
XLA Ops:
  0.0 280.8 %shard_map.55 = bf16[512,2048]{1,0:T(8,128)(2,1)} custom-call(s32[1,1024]{1,0:T(1,128)} %sel_ref.1, f32[1,1024]{1,0:T(1,128)} %gate_ref.1, bf16[512,2048]{1,0:T(8,128)(2,1)} %tok_hbm.1, bf16[2048,768]{1,0:T(8,128)(2,1)} %bitcast.2, bf16[768,2048]{1,0:T(8,128)(2,1)} %bitcast.3), custom_call_target="tpu_custom_call" | custom-call | tf_op jit(solution)/shard_map/pallas_call | solution.py:179
  280.8 3.2 %copy.7 = bf16[512,2048]{1,0:T(8,128)(2,1)} copy(bf16[512,2048]{1,0:T(8,128)(2,1)} %shard_map.55) | data formatting | bytes 4194304

commit v3 on v2

--- a/solution.py
+++ b/solution.py
@@ -18,8 +18,9 @@
 
 
 def moe_kernel(n, sel_ref, gate_ref, tok_hbm, win_hbm, wout_hbm, out_ref,
-               tok, win, wout, ask_out, ask_in, gates, rows_out, rows_in, back_out, back_in, acc,
-               load_sem, ask_send, ask_recv, rows_send, rows_recv, back_send, back_recv):
+               tok, win, wout, ask_out, ask_in, gates, rows_out, rows_in, back_in, relay_a, relay_b, acc,
+               load_sem, ask_send, ask_recv, rows_send, rows_recv, back_send, back_recv,
+               relay_a_recv, relay_b_recv, pass_send):
     me = lax.axis_index("ep")
     groups = n // PEERS
     pair_cap = LANES // PEERS
@@ -36,28 +37,67 @@
     ys = min(4, n // 8)
     zs = n // (8 * ys)
 
-    def partner(j, i, sign):
-        t, core = i // 2, i % 2
-        y_shift, z_shift = j % ys + t, j // ys + 4 - t
-        x = (me // 2 + 4 + sign * t) % 4
-        y = (me // 8 + 8 + sign * y_shift) % ys
-        z = (me // (8 * ys) + 8 + sign * z_shift) % zs
+    def device(offset, sign):
+        dx, dy, dz, core = offset
+        x = (me // 2 + 16 + sign * dx) % 4
+        y = (me // 8 + 16 + sign * dy) % ys
+        z = (me // (8 * ys) + 16 + sign * dz) % zs
         return ((z * ys + y) * 4 + x) * 2 + (me + core) % 2
 
-    def push(src, dst, j, i, peer, index, send_sem, recv_sem):
-        def remote():
+    def offset_of(j, i):
+        t = i // 2
+        return t, (j % ys + t) % ys, (j // ys + 4 - t) % zs, i % 2
+
+    def halfway(d):
+        return (d // 2) * (1 - d % 2)
+
+    def legs(offset, half):
+        core = offset[3]
+        first = [(1 - 2 * half) * halfway(d) + half * (d % 2) * d for d in offset[:3]]
+        rest = [d - f for d, f in zip(offset[:3], first)]
+        return (*first, half * core), (*rest, (1 - half) * core)
+
+    def relayed(offset):
+        return halfway(offset[0]) + halfway(offset[1]) + halfway(offset[2])
+
+    def halves(model_dim):
+        return [pl.ds(h * (model_dim // 2), model_dim // 2) for h in range(2)]
+
+    def send(src, dst, relay, j, i, sign, send_sem, recv_sem, relay_recv):
+        slot = j * PEERS + i
+        offset = offset_of(j, i)
+
+        @pl.when((relayed(offset) == 0) & (slot > 0))
+        def _():
             pltpu.make_async_remote_copy(
-                src_ref=src.at[index], dst_ref=dst.at[j * PEERS + i], send_sem=send_sem, recv_sem=recv_sem,
-                device_id={"ep": peer}, device_id_type=MESH).start()
-
-        def local():
-            pltpu.make_async_copy(src.at[index], dst.at[j * PEERS + i], recv_sem).start()
-
-        if i > 0:
-            remote()
-        else:
-            pl.when(j > 0)(remote)
-            pl.when(j == 0)(local)
+                src_ref=src.at[slot], dst_ref=dst.at[slot], send_sem=send_sem, recv_sem=recv_sem.at[j],
+                device_id={"ep": device(offset, sign)}, device_id_type=MESH).start()
+
+        @pl.when(relayed(offset) > 0)
+        def _():
+            for half, columns in enumerate(halves(model_dim)):
+                pltpu.make_async_remote_copy(
+                    src_ref=src.at[slot, :, columns], dst_ref=relay.at[slot, :, columns],
+                    send_sem=send_sem, recv_sem=relay_recv.at[slot],
+                    device_id={"ep": device(legs(offset, half)[0], sign)}, device_id_type=MESH).start()
+
+        if i == 0:
+            @pl.when(slot == 0)
+            def _():
+                pltpu.make_async_copy(src.at[slot], dst.at[slot], recv_sem.at[j]).start()
+
+    def forward(relay, dst, j, i, sign, pass_send, recv_sem, relay_recv):
+        slot = j * PEERS + i
+        offset = offset_of(j, i)
+
+        @pl.when(relayed(offset) > 0)
+        def _():
+            pltpu.make_async_copy(relay.at[slot], relay.at[slot], relay_recv.at[slot]).wait()
+            for half, columns in enumerate(halves(model_dim)):
+                pltpu.make_async_remote_copy(
+                    src_ref=relay.at[slot, :, columns], dst_ref=dst.at[slot, :, columns],
+                    send_sem=pass_send, recv_sem=recv_sem.at[j],
+                    device_id={"ep": device(legs(offset, half)[1], sign)}, device_id_type=MESH).start()
 
     barrier = pltpu.get_barrier_semaphore()
 
@@ -93,8 +133,16 @@
     @pl.loop(0, groups)
     def _(j):
         for i in range(PEERS):
-            push(ask_out, ask_in, j, i, partner(j, i, -1), partner(j, i, -1), ask_send, ask_recv)
-
+            slot = j * PEERS + i
+            peer = device(offset_of(j, i), -1)
+
+            @pl.when(slot > 0)
+            def _():
+                pltpu.make_async_remote_copy(
+                    src_ref=ask_out.at[peer], dst_ref=ask_in.at[slot], send_sem=ask_send, recv_sem=ask_recv,
+                    device_id={"ep": peer}, device_id_type=MESH).start()
+
+    pltpu.make_async_copy(ask_out.at[me], ask_in.at[0], ask_recv).start()
     pltpu.make_async_copy(ask_in, ask_in, ask_recv).wait()
     for load in loads:
         load.wait()
@@ -125,7 +173,12 @@
             got = _dot(pick, tok[:, c:c + 512]).astype(jnp.bfloat16)
             rows_out[pl.ds(j * PEERS, PEERS), :, c:c + 512] = got.reshape(PEERS, pair_cap, 512)
         for i in range(PEERS):
-            push(rows_out, rows_in, j, i, partner(j, i, 1), j * PEERS + i, rows_send, rows_recv.at[j])
+            send(rows_out, rows_in, relay_a, j, i, 1, rows_send, rows_recv, relay_a_recv)
+
+    @pl.loop(0, groups)
+    def _(j):
+        for i in range(PEERS):
+            forward(relay_a, rows_in, j, i, 1, pass_send, rows_recv, relay_a_recv)
 
     @pl.loop(0, groups)
     def _(j):
@@ -133,15 +186,20 @@
         first = pl.ds(j * PEERS, PEERS)
         x = rows_in[first].reshape(LANES, model_dim)
         hidden = jax.nn.gelu(_dot(x, win[...]), approximate=True).astype(jnp.bfloat16)
-        lines = [gates[partner(j, i, -1)] for i in range(PEERS)]
+        lines = [gates[device(offset_of(j, i), -1)] for i in range(PEERS)]
         scale = column(lane_row(jnp.concatenate(lines, axis=0)))
         scale = jnp.concatenate([scale] * (512 // LANES), axis=1)
         for c in range(0, model_dim, 512):
             o = _dot(hidden, wout[:, c:c + 512])
             p = jnp.where(scale > 0.0, scale * o, 0.0).astype(jnp.bfloat16)
-            back_out[first, :, c:c + 512] = p.reshape(PEERS, pair_cap, 512)
-        for i in range(PEERS):
-            push(back_out, back_in, j, i, partner(j, i, -1), j * PEERS + i, back_send, back_recv.at[j])
+            rows_in[first, :, c:c + 512] = p.reshape(PEERS, pair_cap, 512)
+        for i in range(PEERS):
+            send(rows_in, back_in, relay_b, j, i, -1, back_send, back_recv, relay_b_recv)
+
+    @pl.loop(0, groups)
+    def _(j):
+        for i in range(PEERS):
+            forward(relay_b, back_in, j, i, -1, pass_send, back_recv, relay_b_recv)
 
     token_ids = lax.broadcasted_iota(jnp.int32, (tok_count, LANES), 0).astype(jnp.float32) + 1.0
 
@@ -159,9 +217,13 @@
     for c in range(0, model_dim, 512):
         out_ref[:, c:c + 512] = acc[:, c:c + 512].astype(out_ref.dtype)
 
-    for src, send_sem in ((ask_out, ask_send), (rows_out, rows_send), (back_out, back_send)):
+    for src, send_sem in ((ask_out, ask_send), (rows_out, rows_send), (rows_in, back_send)):
         sent = src.at[pl.ds(0, n - 1)]
         pltpu.make_async_copy(sent, sent, send_sem).wait()
+    straight = (4 - 1) * (ys - ys // 4) * (zs - zs // 4) * 2
+    for relay in (relay_a, relay_b):
+        sent = relay.at[pl.ds(0, n - straight)]
+        pltpu.make_async_copy(sent, sent, pass_send).wait()
 
 
 def solution(mesh):
@@ -188,7 +250,7 @@
                 pltpu.VMEM((n, 1, LANES), jnp.float32),
                 pltpu.VMEM((n, 1, LANES), jnp.float32),
                 pltpu.VMEM((n, 1, LANES), jnp.float32),
-                blocks, blocks, blocks, blocks,
+                blocks, blocks, blocks, blocks, blocks,
                 pltpu.VMEM((tok_count, model_dim), jnp.float32),
                 pltpu.SemaphoreType.DMA((3,)),
                 pltpu.SemaphoreType.DMA,
@@ -197,6 +259,9 @@
                 pltpu.SemaphoreType.DMA((n // PEERS,)),
                 pltpu.SemaphoreType.DMA,
                 pltpu.SemaphoreType.DMA((n // PEERS,)),
+                pltpu.SemaphoreType.DMA((n,)),
+                pltpu.SemaphoreType.DMA((n,)),
+                pltpu.SemaphoreType.DMA,
             ],
             compiler_params=pltpu.CompilerParams(
                 collective_id=0, has_side_effects=True, vmem_limit_bytes=63 * 1024 * 1024),

time: 284 us -> 261 us (0.919)
  the two profiles are of different devices: /device:TPU:83 before, /device:TPU:102 now
where the time goes in v3:
time: 261 us
  Pallas kernels  257 us (98%)
  local copies, waits for them, and re-layouts  3.16 us (1%)
    pallas_call x1, Pallas kernels, local_layer(): pl.pallas_call(functools.partial(moe_kernel, n), out_shape=jax.ShapeDtype...  257 us

profile of v3, /device:TPU:102, one launch (start us, length us, event | category | flops | bytes accessed | tf_op | source)
XLA Modules:
  0.0 260.5 jit_solution(5869907206042498992)
XLA Ops:
  0.0 257.3 %shard_map.55 = bf16[512,2048]{1,0:T(8,128)(2,1)} custom-call(s32[1,1024]{1,0:T(1,128)} %sel_ref.1, f32[1,1024]{1,0:T(1,128)} %gate_ref.1, bf16[512,2048]{1,0:T(8,128)(2,1)} %tok_hbm.1, bf16[2048,768]{1,0:T(8,128)(2,1)} %bitcast.2, bf16[768,2048]{1,0:T(8,128)(2,1)} %bitcast.3), custom_call_target="tpu_custom_call" | custom-call | tf_op jit(solution)/shard_map/pallas_call | solution.py:241
  257.4 3.2 %copy.7 = bf16[512,2048]{1,0:T(8,128)(2,1)} copy(bf16[512,2048]{1,0:T(8,128)(2,1)} %shard_map.55) | data formatting | bytes 4194304

commit v4 on v3

--- a/solution.py
+++ b/solution.py
@@ -48,17 +48,13 @@
         t = i // 2
         return t, (j % ys + t) % ys, (j // ys + 4 - t) % zs, i % 2
 
-    def halfway(d):
-        return (d // 2) * (1 - d % 2)
-
     def legs(offset, half):
-        core = offset[3]
-        first = [(1 - 2 * half) * halfway(d) + half * (d % 2) * d for d in offset[:3]]
-        rest = [d - f for d, f in zip(offset[:3], first)]
-        return (*first, half * core), (*rest, (1 - half) * core)
+        dx, dy, dz, core = offset
+        pair = (dx, 0, 0, 0), (0, dy, dz, core)
+        return pair[::-1] if half else pair
 
     def relayed(offset):
-        return halfway(offset[0]) + halfway(offset[1]) + halfway(offset[2])
+        return offset[0] * (offset[1] + offset[2])
 
     def halves(model_dim):
         return [pl.ds(h * (model_dim // 2), model_dim // 2) for h in range(2)]
@@ -206,12 +202,15 @@
     for c in range(0, model_dim, 512):
         acc[:, c:c + 512] = tok[:, c:c + 512].astype(jnp.float32)
 
-    @pl.loop(0, groups)
-    def _(j):
-        put = (token_ids == asked(j)).astype(jnp.bfloat16)
-        arrived(back_in, j, back_recv)
+    @pl.loop(0, groups // 2)
+    def _(pair):
+        put = []
+        for j in (2 * pair, 2 * pair + 1):
+            put.append((token_ids == asked(j)).astype(jnp.bfloat16))
+            arrived(back_in, j, back_recv)
+        put = jnp.concatenate(put, axis=1)
         for c in range(0, model_dim, 512):
-            p = back_in[pl.ds(j * PEERS, PEERS), :, c:c + 512].reshape(LANES, 512)
+            p = back_in[pl.ds(pair * 2 * PEERS, 2 * PEERS), :, c:c + 512].reshape(2 * LANES, 512)
             acc[:, c:c + 512] += _dot(put, p)
 
     for c in range(0, model_dim, 512):
@@ -220,9 +219,9 @@
     for src, send_sem in ((ask_out, ask_send), (rows_out, rows_send), (rows_in, back_send)):
         sent = src.at[pl.ds(0, n - 1)]
         pltpu.make_async_copy(sent, sent, send_sem).wait()
-    straight = (4 - 1) * (ys - ys // 4) * (zs - zs // 4) * 2
+    turns = (4 - 1) * (ys * zs - 1) * 2
     for relay in (relay_a, relay_b):
-        sent = relay.at[pl.ds(0, n - straight)]
+        sent = relay.at[pl.ds(0, turns)]
         pltpu.make_async_copy(sent, sent, pass_send).wait()
 
 

time: 261 us -> 253 us (0.969)
  the two profiles are of different devices: /device:TPU:102 before, /device:TPU:15 now
where the time goes in v4:
time: 253 us
  Pallas kernels  250 us (99%)
  local copies, waits for them, and re-layouts  3.16 us (1%)
    pallas_call x1, Pallas kernels, local_layer(): pl.pallas_call(functools.partial(moe_kernel, n), out_shape=jax.ShapeDtype...  250 us

profile of v4, /device:TPU:15, one launch (start us, length us, event | category | flops | bytes accessed | tf_op | source)
XLA Modules:
  0.0 253.1 jit_solution(5930638179184258973)
XLA Ops:
  0.0 249.9 %shard_map.55 = bf16[512,2048]{1,0:T(8,128)(2,1)} custom-call(s32[1,1024]{1,0:T(1,128)} %sel_ref.1, f32[1,1024]{1,0:T(1,128)} %gate_ref.1, bf16[512,2048]{1,0:T(8,128)(2,1)} %tok_hbm.1, bf16[2048,768]{1,0:T(8,128)(2,1)} %bitcast.2, bf16[768,2048]{1,0:T(8,128)(2,1)} %bitcast.3), custom_call_target="tpu_custom_call" | custom-call | tf_op jit(solution)/shard_map/pallas_call | solution.py:240
  249.9 3.2 %copy.7 = bf16[512,2048]{1,0:T(8,128)(2,1)} copy(bf16[512,2048]{1,0:T(8,128)(2,1)} %shard_map.55) | data formatting | bytes 4194304

commit v5 on v4

--- a/solution.py
+++ b/solution.py
@@ -18,14 +18,16 @@
 
 
 def moe_kernel(n, sel_ref, gate_ref, tok_hbm, win_hbm, wout_hbm, out_ref,
-               tok, win, wout, ask_out, ask_in, gates, rows_out, rows_in, back_in, relay_a, relay_b, acc,
+               tok, win, wout, ask_out, ask_in, gates, rows_out, rows_in, relay_a, relay_b, acc,
                load_sem, ask_send, ask_recv, rows_send, rows_recv, back_send, back_recv,
-               relay_a_recv, relay_b_recv, pass_send):
+               relay_a_recv, relay_b_recv, pass_send, ready):
     me = lax.axis_index("ep")
     groups = n // PEERS
     pair_cap = LANES // PEERS
     tok_count, model_dim = tok.shape
     slots = sel_ref.shape[1]
+
+    back_in = rows_out
 
     loads = [
         pltpu.make_async_copy(src, dst, load_sem.at[i])
@@ -34,7 +36,7 @@
     for load in loads:
         load.start()
 
-    ys = min(4, n // 8)
+    ys = 4 if n >= 128 else 2
     zs = n // (8 * ys)
 
     def device(offset, sign):
@@ -48,52 +50,68 @@
         t = i // 2
         return t, (j % ys + t) % ys, (j // ys + 4 - t) % zs, i % 2
 
-    def legs(offset, half):
-        dx, dy, dz, core = offset
-        pair = (dx, 0, 0, 0), (0, dy, dz, core)
-        return pair[::-1] if half else pair
-
-    def relayed(offset):
-        return offset[0] * (offset[1] + offset[2])
-
-    def halves(model_dim):
-        return [pl.ds(h * (model_dim // 2), model_dim // 2) for h in range(2)]
-
-    def send(src, dst, relay, j, i, sign, send_sem, recv_sem, relay_recv):
+    def nonzero(d):
+        return (d + 3) // 4
+
+    def axes(offset):
+        return sum(nonzero(d) for d in offset[:3])
+
+    def way(offset, half):
+        order = (2, 1, 0) if half else (0, 1, 2)
+        a, b, c = (offset[k] for k in order)
+        na, nb, nc = nonzero(a), nonzero(b), nonzero(c)
+        first = a, (1 - na) * b, 0
+        middle = 0, b, 0
+        last = 0, (1 - nc) * b, c
+
+        def placed(leg, core):
+            return (*(leg[order.index(k)] for k in range(3)), core)
+
+        return placed(first, 0), placed(middle, 0), placed(last, offset[3])
+
+    halves = [pl.ds(h * (model_dim // 2), model_dim // 2) for h in range(2)]
+
+    def hop(src, dst, slot, half, leg, sign, send_sem, recv_sem):
+        pltpu.make_async_remote_copy(
+            src_ref=src.at[slot, :, halves[half]], dst_ref=dst.at[slot, :, halves[half]], send_sem=send_sem, recv_sem=recv_sem,
+            device_id={"ep": device(leg, sign)}, device_id_type=MESH).start()
+
+    def take(relay, slot, half, recv_sem):
+        part = relay.at[slot, :, halves[half]]
+        pltpu.make_async_copy(part, part, recv_sem.at[half * n + slot]).wait()
+
+    def straight(src, dst, j, i, sign, send_sem, recv_sem):
         slot = j * PEERS + i
         offset = offset_of(j, i)
 
-        @pl.when((relayed(offset) == 0) & (slot > 0))
+        @pl.when((axes(offset) < 2) & (slot > 0))
         def _():
             pltpu.make_async_remote_copy(
                 src_ref=src.at[slot], dst_ref=dst.at[slot], send_sem=send_sem, recv_sem=recv_sem.at[j],
                 device_id={"ep": device(offset, sign)}, device_id_type=MESH).start()
 
-        @pl.when(relayed(offset) > 0)
-        def _():
-            for half, columns in enumerate(halves(model_dim)):
-                pltpu.make_async_remote_copy(
-                    src_ref=src.at[slot, :, columns], dst_ref=relay.at[slot, :, columns],
-                    send_sem=send_sem, recv_sem=relay_recv.at[slot],
-                    device_id={"ep": device(legs(offset, half)[0], sign)}, device_id_type=MESH).start()
-
         if i == 0:
             @pl.when(slot == 0)
             def _():
                 pltpu.make_async_copy(src.at[slot], dst.at[slot], recv_sem.at[j]).start()
 
-    def forward(relay, dst, j, i, sign, pass_send, recv_sem, relay_recv):
+    def left(src, count, send_sem):
+        if count > 0:
+            sent = src.at[pl.ds(0, count)]
+            pltpu.make_async_copy(sent, sent, send_sem).wait()
+
+    def relays_left():
+        left(relay_a, n - 2 * (1 + 3 + ys - 1 + zs - 1), pass_send)
+        left(relay_b, 3 * (ys - 1) * (zs - 1) * 2, pass_send)
+
+    def each_half(j, i, bends, body):
         slot = j * PEERS + i
         offset = offset_of(j, i)
-
-        @pl.when(relayed(offset) > 0)
-        def _():
-            pltpu.make_async_copy(relay.at[slot], relay.at[slot], relay_recv.at[slot]).wait()
-            for half, columns in enumerate(halves(model_dim)):
-                pltpu.make_async_remote_copy(
-                    src_ref=relay.at[slot, :, columns], dst_ref=dst.at[slot, :, columns],
-                    send_sem=pass_send, recv_sem=recv_sem.at[j],
-                    device_id={"ep": device(legs(offset, half)[1], sign)}, device_id_type=MESH).start()
+        if offset[0] > 0 or bends < 2:
+            @pl.when(axes(offset) == bends + 1)
+            def _():
+                for half in range(2):
+                    body(slot, half, way(offset, half))
 
     barrier = pltpu.get_barrier_semaphore()
 
@@ -169,12 +187,44 @@
             got = _dot(pick, tok[:, c:c + 512]).astype(jnp.bfloat16)
             rows_out[pl.ds(j * PEERS, PEERS), :, c:c + 512] = got.reshape(PEERS, pair_cap, 512)
         for i in range(PEERS):
-            send(rows_out, rows_in, relay_a, j, i, 1, rows_send, rows_recv, relay_a_recv)
-
-    @pl.loop(0, groups)
-    def _(j):
-        for i in range(PEERS):
-            forward(relay_a, rows_in, j, i, 1, pass_send, rows_recv, relay_a_recv)
+            straight(rows_out, rows_in, j, i, 1, rows_send, rows_recv)
+
+            def start(slot, half, legs):
+                hop(rows_out, relay_a, slot, half, legs[0], 1, rows_send, relay_a_recv.at[half * n + slot])
+
+            each_half(j, i, 1, start)
+            each_half(j, i, 2, start)
+
+    @pl.loop(0, groups)
+    def _(j):
+        for i in range(PEERS):
+            def finish(slot, half, legs):
+                take(relay_a, slot, half, relay_a_recv)
+                hop(relay_a, rows_in, slot, half, legs[2], 1, pass_send, rows_recv.at[j])
+
+            def turn(slot, half, legs):
+                take(relay_a, slot, half, relay_a_recv)
+                hop(relay_a, relay_b, slot, half, legs[1], 1, pass_send, relay_b_recv.at[half * n + slot])
+
+            each_half(j, i, 1, finish)
+            each_half(j, i, 2, turn)
+
+    @pl.loop(0, groups)
+    def _(j):
+        for i in range(PEERS):
+            def finish(slot, half, legs):
+                take(relay_b, slot, half, relay_b_recv)
+                hop(relay_b, rows_in, slot, half, legs[2], 1, pass_send, rows_recv.at[j])
+
+            each_half(j, i, 2, finish)
+
+    left(rows_out, n - 1, rows_send)
+    relays_left()
+    writers = [(0, 0, 0, 1)]
+    for axis, size in enumerate((4, ys, zs)):
+        writers += [tuple(d if k == axis else 0 for k in range(3)) + (core,) for d in range(1, size) for core in range(2)]
+    for offset in writers:
+        pl.semaphore_signal(ready, inc=1, device_id={"ep": device(offset, 1)}, device_id_type=MESH)
 
     @pl.loop(0, groups)
     def _(j):
@@ -189,13 +239,45 @@
             o = _dot(hidden, wout[:, c:c + 512])
             p = jnp.where(scale > 0.0, scale * o, 0.0).astype(jnp.bfloat16)
             rows_in[first, :, c:c + 512] = p.reshape(PEERS, pair_cap, 512)
-        for i in range(PEERS):
-            send(rows_in, back_in, relay_b, j, i, -1, back_send, back_recv, relay_b_recv)
-
-    @pl.loop(0, groups)
-    def _(j):
-        for i in range(PEERS):
-            forward(relay_b, back_in, j, i, -1, pass_send, back_recv, relay_b_recv)
+
+        @pl.when(j == 0)
+        def _():
+            pl.semaphore_wait(ready, len(writers))
+
+        for i in range(PEERS):
+            straight(rows_in, back_in, j, i, -1, back_send, back_recv)
+
+            def start(slot, half, legs):
+                hop(rows_in, relay_a, slot, half, legs[2], -1, back_send, relay_a_recv.at[half * n + slot])
+
+            def start_far(slot, half, legs):
+                hop(rows_in, relay_b, slot, half, legs[2], -1, back_send, relay_b_recv.at[half * n + slot])
+
+            each_half(j, i, 1, start)
+            each_half(j, i, 2, start_far)
+
+    @pl.loop(0, groups)
+    def _(j):
+        for i in range(PEERS):
+            def finish(slot, half, legs):
+                take(relay_a, slot, half, relay_a_recv)
+                hop(relay_a, back_in, slot, half, legs[0], -1, pass_send, back_recv.at[j])
+
+            def turn(slot, half, legs):
+                take(relay_b, slot, half, relay_b_recv)
+                hop(relay_b, relay_a, slot, half, legs[1], -1, pass_send, relay_a_recv.at[half * n + slot])
+
+            each_half(j, i, 1, finish)
+            each_half(j, i, 2, turn)
+
+    @pl.loop(0, groups)
+    def _(j):
+        for i in range(PEERS):
+            def finish(slot, half, legs):
+                take(relay_a, slot, half, relay_a_recv)
+                hop(relay_a, back_in, slot, half, legs[0], -1, pass_send, back_recv.at[j])
+
+            each_half(j, i, 2, finish)
 
     token_ids = lax.broadcasted_iota(jnp.int32, (tok_count, LANES), 0).astype(jnp.float32) + 1.0
 
@@ -216,13 +298,9 @@
     for c in range(0, model_dim, 512):
         out_ref[:, c:c + 512] = acc[:, c:c + 512].astype(out_ref.dtype)
 
-    for src, send_sem in ((ask_out, ask_send), (rows_out, rows_send), (rows_in, back_send)):
-        sent = src.at[pl.ds(0, n - 1)]
-        pltpu.make_async_copy(sent, sent, send_sem).wait()
-    turns = (4 - 1) * (ys * zs - 1) * 2
-    for relay in (relay_a, relay_b):
-        sent = relay.at[pl.ds(0, turns)]
-        pltpu.make_async_copy(sent, sent, pass_send).wait()
+    left(ask_out, n - 1, ask_send)
+    left(rows_in, n - 1, back_send)
+    relays_left()
 
 
 def solution(mesh):
@@ -249,7 +327,7 @@
                 pltpu.VMEM((n, 1, LANES), jnp.float32),
                 pltpu.VMEM((n, 1, LANES), jnp.float32),
                 pltpu.VMEM((n, 1, LANES), jnp.float32),
-                blocks, blocks, blocks, blocks, blocks,
+                blocks, blocks, blocks, blocks,
                 pltpu.VMEM((tok_count, model_dim), jnp.float32),
                 pltpu.SemaphoreType.DMA((3,)),
                 pltpu.SemaphoreType.DMA,
@@ -258,9 +336,10 @@
                 pltpu.SemaphoreType.DMA((n // PEERS,)),
                 pltpu.SemaphoreType.DMA,
                 pltpu.SemaphoreType.DMA((n // PEERS,)),
-                pltpu.SemaphoreType.DMA((n,)),
-                pltpu.SemaphoreType.DMA((n,)),
-                pltpu.SemaphoreType.DMA,
+                pltpu.SemaphoreType.DMA((2 * n,)),
+                pltpu.SemaphoreType.DMA((2 * n,)),
+                pltpu.SemaphoreType.DMA,
+                pltpu.SemaphoreType.REGULAR,
             ],
             compiler_params=pltpu.CompilerParams(
                 collective_id=0, has_side_effects=True, vmem_limit_bytes=63 * 1024 * 1024),

time: 253 us -> 225 us (0.89)
  the two profiles are of different devices: /device:TPU:15 before, /device:TPU:12 now
where the time goes in v5:
time: 225 us; the launch traced here: 222 us
  Pallas kernels  219 us (97%)
  local copies, waits for them, and re-layouts  3.16 us (1%)
    pallas_call x1, Pallas kernels, local_layer(): pl.pallas_call(functools.partial(moe_kernel, n), out_shape=jax.ShapeDtype...  219 us

profile of v5, /device:TPU:12, one launch (start us, length us, event | category | flops | bytes accessed | tf_op | source)
XLA Modules:
  0.0 222.0 jit_solution(15575618955122723165)
XLA Ops:
  0.0 218.8 %shard_map.55 = bf16[512,2048]{1,0:T(8,128)(2,1)} custom-call(s32[1,1024]{1,0:T(1,128)} %sel_ref.1, f32[1,1024]{1,0:T(1,128)} %gate_ref.1, bf16[512,2048]{1,0:T(8,128)(2,1)} %tok_hbm.1, bf16[2048,768]{1,0:T(8,128)(2,1)} %bitcast.2, bf16[768,2048]{1,0:T(8,128)(2,1)} %bitcast.3), custom_call_target="tpu_custom_call" | custom-call | tf_op jit(solution)/shard_map/pallas_call | solution.py:318
  218.8 3.2 %copy.7 = bf16[512,2048]{1,0:T(8,128)(2,1)} copy(bf16[512,2048]{1,0:T(8,128)(2,1)} %shard_map.55) | data formatting | bytes 4194304
